TPU v7x, 32 devices: a whole 2x2x4 slice. The times are simulated.
32 devices in a mesh: shot: 4 (over y, core), space: 8 (over z, x).
Axes of the slice: x: 2, y: 2, z: 4, core: 2. Of those that a mesh axis runs over, the one named last changes fastest.
Arguments:
- adjoint_now: float32 [4, 128, 64, 512], P('shot', 'space'), may hold values from -6 to 6
- adjoint_later: float32 [4, 128, 64, 512], P('shot', 'space'), may hold values from -6 to 6
- courant: float32 [128, 64, 512], P('space'), may hold values from 0.05 to 0.2
- checkpoint_codes: int32 [4, 6, 128, 64, 128], P('shot', None, 'space'), may hold values from -2147483648 to 2147483646
- scale_index: int32 [4, 6, 128, 256], P('shot', None, 'space'), may hold values from 0 to 63
- scale_table: float32 [64], replicated, may hold values from 0.001 to 0.01
- receiver_cell: int32 [4, 2048], P('shot', 'space'), may hold values from 0 to 4194303, as said below
- observed: float32 [4, 4, 2048], P('shot', None, 'space'), may hold values from -12 to 12
- source_cell: int32 [4, 3], P('shot'), may hold values from 0 to 511, as said below
Outputs:
- gradient: float32 [128, 64, 512], P('space', 'shot')
- adjoint_first: float32 [4, 128, 64, 512], P('shot', 'space')
- adjoint_second: float32 [4, 128, 64, 512], P('shot', 'space')
- misfit: float32 [], replicated
Inputs may be any that keep to these rules, and one draw needn't show every extreme that they name: `receiver_cell`: for every r, entries r * 256 to (r + 1) * 256 - 1 of each shot's row are flat indices (z * 64 + y) * 512 + x of cells with r * 16 <= z < (r + 1) * 16. `source_cell`: column 0 is a z index below 128, column 1 a y index below 64, column 2 an x index below 512.
All inputs are finite; a program needn't handle non-finite values.
Results may differ from a plain program's by a relative error of at most 0.0001.
Values sent between devices are 32-bit elements; how exact they have to be, the bound alone decides.
A program may use at most 128 MiB of HBM per device.

v0:
```python
import jax
import jax.numpy as jnp
from jax import lax
from jax.sharding import PartitionSpec as P

ITERS = 4
QBLOCK = 128
MUTE = 8
COEFFS = (-205.0 / 72.0, 8.0 / 5.0, -1.0 / 5.0, 8.0 / 315.0, -1.0 / 560.0)


def with_halo(block, sides, width):
    for axis, dim in sides:
        count = lax.axis_size(axis)
        forward = [(i, i + 1) for i in range(count - 1)]
        backward = [(target, source) for source, target in forward]
        low = lax.ppermute(
            lax.slice_in_dim(block, block.shape[dim] - width, None, axis=dim), axis, forward
        )
        high = lax.ppermute(lax.slice_in_dim(block, 0, width, axis=dim), axis, backward)
        block = jnp.concatenate([low, block, high], axis=dim)
    return block


def decode(words, index, table):
    planes = [jnp.bitwise_and(jnp.right_shift(words, 8 * m), 255) for m in range(4)]
    codes = jnp.concatenate(planes, axis=-1)
    centred = (codes - 128).astype(jnp.float32)
    depth, rows, cols = centred.shape
    onehot = index[..., None] == jnp.arange(table.shape[0], dtype=jnp.int32)
    scale = jnp.sum(jnp.where(onehot, table, 0.0), axis=-1)
    blocks = centred.reshape(depth, rows, cols // QBLOCK, QBLOCK) * scale.reshape(
        depth, rows, cols // QBLOCK, 1
    )
    return blocks.reshape(depth, rows, cols)


def laplace(field):
    depth, rows, cols = field.shape
    deep = with_halo(field, (("space", 0),), 4)
    flat = jnp.pad(field, ((0, 0), (4, 4), (4, 4)))
    total = 3.0 * COEFFS[0] * field
    for step in range(1, 5):
        total = total + COEFFS[step] * (
            deep[4 + step : 4 + step + depth] + deep[4 - step : 4 - step + depth]
        )
        total = total + COEFFS[step] * (
            flat[:, 4 + step : 4 + step + rows, 4 : 4 + cols]
            + flat[:, 4 - step : 4 - step + rows, 4 : 4 + cols]
        )
        total = total + COEFFS[step] * (
            flat[:, 4 : 4 + rows, 4 + step : 4 + step + cols]
            + flat[:, 4 : 4 + rows, 4 - step : 4 - step + cols]
        )
    return total


def body(
    adjoint_now,
    adjoint_later,
    courant,
    checkpoint_codes,
    scale_index,
    scale_table,
    receiver_cell,
    observed,
    source_cell,
):
    now = adjoint_now[0]
    later = adjoint_later[0]
    depth, rows, cols = now.shape
    first_z = lax.axis_index("space") * depth
    cells = receiver_cell[0] - first_z * (rows * cols)
    fields = [
        decode(checkpoint_codes[0, level], scale_index[0, level], scale_table)
        for level in range(ITERS + 2)
    ]
    image = jnp.zeros((depth, rows, cols), jnp.float32)
    misfit_part = jnp.zeros((), jnp.float32)
    for step in range(ITERS):
        level = ITERS - step
        synthetic = jnp.take(fields[level].reshape(-1), cells)
        residual = synthetic - observed[0, level - 1]
        misfit_part = misfit_part + jnp.sum(residual * residual)
        image = image + now * (fields[level + 1] - 2.0 * fields[level] + fields[level - 1])
        stepped = 2.0 * now - later + courant * laplace(now)
        stepped = stepped.reshape(-1).at[cells].add(residual).reshape(depth, rows, cols)
        later = now
        now = stepped
    source = source_cell[0]
    zpos = (first_z + jnp.arange(depth, dtype=jnp.int32)).reshape(depth, 1, 1)
    ypos = jnp.arange(rows, dtype=jnp.int32).reshape(1, rows, 1)
    xpos = jnp.arange(cols, dtype=jnp.int32).reshape(1, 1, cols)
    dist = ((zpos - source[0]) ** 2 + (ypos - source[1]) ** 2 + (xpos - source[2]) ** 2).astype(
        jnp.float32
    )
    muted = image * (1.0 - jnp.exp(-dist / (2.0 * MUTE * MUTE)))
    gradient = lax.psum_scatter(muted, "shot", scatter_dimension=1, tiled=True)
    count = lax.axis_size("shot") * ITERS * receiver_cell.shape[1] * lax.axis_size("space")
    misfit = 0.5 * lax.psum(misfit_part, ("shot", "space")) / count
    return (gradient, now[None], later[None], misfit)


def solution(mesh):
    placed = (
        P("shot", "space", None, None),
        P("shot", "space", None, None),
        P("space", None, None),
        P("shot", None, "space", None, None),
        P("shot", None, "space", None),
        P(),
        P("shot", "space"),
        P("shot", None, "space"),
        P("shot", None),
    )
    return jax.shard_map(
        body,
        mesh=mesh,
        in_specs=placed,
        out_specs=(
            P("space", "shot", None),
            P("shot", "space", None, None),
            P("shot", "space", None, None),
            P(),
        ),
        check_vma=False,
    )
```

profile of v0, /device:TPU:0, one launch (start us, length us, event | category | flops | bytes accessed | tf_op | source)
XLA Modules:
  0.0 308.4 jit_solution(9114764034815318383)
XLA Ops:
  7.2 2.3 slice_bitcast_fusion.1
  10.8 6.3 %collective-permute-start.1 = (f32[4,64,512]{2,1,0:T(8,128)}, f32[4,64,512]{2,1,0:T(8,128)}, u32[]{:S(2)}, u32[]{:S(2)}) collective-permute-start(f32[4,64,512]{2,1,0:T(8,128)} %get-tuple-element.59), channel_id=1, source_target_pairs={{0,1},{1,2},{2,3},{3,4},{4,5},{5,6},{6,7},{8,9},{9,10},{10,11},{11... | collective-permute-start | bytes 1572872 | tf_op jit(solution)/shard_map/ppermute | solution.py:17
  17.1 3.3 %and_bitcast_fusion.7 = (s32[16,64,1,128]{3,1,0,2:T(8,128)}, s32[16,64,1,128]{3,1,0,2:T(8,128)}, s32[16,64,1,128]{3,1,0,2:T(8,128)}, s32[16,64,1,128]{3,1,0,2:T(8,128)}, s32[16,64,1,128]{3,1,0,2:T(8,128)S(1)}) fusion(s32[1,6,16,64,128]{4,3,2,1,0:T(8,128)} %param.14), kind=kLoop, calls=%fused_computation.304 | loop fusion | flops 1310720 | bytes 5242880 | tf_op jit(solution)/shard_map/and | solution.py:26
  20.4 3.7 %and_bitcast_fusion.23 = (s32[16,64,1,128]{3,1,0,2:T(8,128)S(1)}, s32[16,64,1,128]{3,1,0,2:T(8,128)}, s32[16,64,1,128]{3,1,0,2:T(8,128)}, s32[16,64,1,128]{3,1,0...) fusion(s32[1,6,16,64,128]{4,3,2,1,0:T(8,128)S(1)} %copy-done.11), kind=kLoop, calls=%fused_computation.322 | loop fusion | flops 4980736 | bytes 13107200 | tf_op jit(solution)/shard_map/and | solution.py:26
  24.2 1.5 select_reduce_fusion.5
  26.5 3.9 %fusion.162 = (f32[16,64,4,128]{3,1,0,2:T(8,128)S(1)}, f32[16,64,4,128]{3,1,0,2:T(8,128)S(1)}) fusion(s32[16,64,1,128]{3,1,0,2:T(8,128)} %get-tuple-element.27, s32[16,64,1,128]{3,1,0,2:T(8,128)} %get-tuple-element.26, s32[16,64,1,128]{3,1,0,2:T(8,128)} %get-tuple-element.25, s32[16,64,1,128]{3,1,0,2:T(8,128)} %get-tuple-element.43, ...), kind=kLoop, calls=%fused_computation.270 | loop fusion | flops 6291456 | bytes 8421376 | tf_op jit(solution)/shard_map/mul | solution.py:32
  30.3 2.8 copy.40
  33.2 2.7 copy.43
  36.0 2.6 fusion.166
  38.6 3.4 %gather_fusion = f32[256]{0:T(256)S(1)} fusion(f32[524288]{0:T(1024)} %bitcast.181, s32[1024]{0:T(1024)S(1)} %pad_clamp_fusion), kind=kCustom, calls=%fused_computation.clone | custom fusion | bytes 3072 | tf_op jit(solution)/shard_map/jit(_take)/gather | solution.py:82
  42.0 3.5 %gather_fusion.1 = f32[256]{0:T(256)S(1)} fusion(f32[524288]{0:T(1024)} %bitcast.182, s32[1024]{0:T(1024)S(1)} %pad_clamp_fusion), kind=kCustom, calls=%fused_computation.1.clone | custom fusion | bytes 3072 | tf_op jit(solution)/shard_map/jit(_take)/gather | solution.py:82
  45.5 2.7 copy.47
  48.2 3.5 %gather_fusion.2 = f32[256]{0:T(256)S(1)} fusion(f32[524288]{0:T(1024)} %bitcast.184, s32[1024]{0:T(1024)S(1)} %pad_clamp_fusion), kind=kCustom, calls=%fused_computation.2.clone | custom fusion | bytes 3072 | tf_op jit(solution)/shard_map/jit(_take)/gather | solution.py:82
  51.7 4.5 %copy.51 = f32[16,64,4,128]{3,2,1,0:T(4,128)} copy(f32[16,64,4,128]{3,1,0,2:T(8,128)} %get-tuple-element.84) | data formatting | bytes 4194304 | tf_op jit(solution)/shard_map/mul | solution.py:32
  56.2 3.5 %gather_fusion.3 = f32[256]{0:T(256)S(1)} fusion(f32[524288]{0:T(1024)} %bitcast.183, s32[1024]{0:T(1024)S(1)} %pad_clamp_fusion), kind=kCustom, calls=%fused_computation.3.clone | custom fusion | bytes 3072 | tf_op jit(solution)/shard_map/jit(_take)/gather | solution.py:82
  60.3 29.2 %fusion.10 = f32[16,64,512]{2,1,0:T(8,128)S(1)} fusion(f32[16,64,512]{2,1,0:T(8,128)S(1)} %copy-done.2, f32[16,64,512]{2,1,0:T(8,128)} %bitcast.173, f32[4,64,512]{2,1,0:T(8,128)} %collective-permute-done.1, f32[4,64,512]{2,1,0:T(8,128)} %collective-permute-done, f32[1,16,64,512]{3,2,1,0:T(8,128)} %param.12), kind=kLoop, calls=%fused_computation.94 | loop fusion | flops 25690112 | bytes 9437184 | tf_op jit(solution)/shard_map/add | solution.py:86
  90.1 2.9 scatter_fusion
  94.2 1.9 slice.517
  96.1 4.8 %collective-permute-start.3 = (f32[4,64,512]{2,1,0:T(8,128)}, f32[4,64,512]{2,1,0:T(8,128)}, u32[]{:S(2)}, u32[]{:S(2)}) collective-permute-start(f32[4,64,512]{2,1,0:T(8,128)} %slice.517), channel_id=1, source_target_pairs={{0,1},{1,2},{2,3},{3,4},{4,5},{5,6},{6,7},{8,9},{9,10},{10,11},{11... | collective-permute-start | bytes 1572872 | tf_op jit(solution)/shard_map/ppermute | solution.py:17
  100.9 1.9 slice.514
  104.2 1.7 reshape.603
  105.9 16.4 %collective-permute-done.3 = f32[4,64,512]{2,1,0:T(8,128)} collective-permute-done((f32[4,64,512]{2,1,0:T(8,128)}, f32[4,64,512]{2,1,0:T(8,128)}, u32[]{:S(2)}, u32[]{:S(2)}) %collective-permute-start.3) | collective-permute-done | bytes 524320 | tf_op jit(solution)/shard_map/ppermute | solution.py:17
  125.8 4.9 %fusion.56 = f32[16,64,512]{2,1,0:T(8,128)S(1)} fusion(f32[16,64,512]{2,1,0:T(8,128)S(1)} %copy-done.3, f32[16,64,512]{2,1,0:T(8,128)S(1)} %reshape.603, f32[20,64,512]{2,1,0:T(8,128)S(1)} %get-tuple-element.57, f32[20,64,512]{2,1,0:T(8,128)S(1)} %constant_dynamic-update-slice_fusion, f32[1,16,64,512]{3,2,1,0:T(8,128)S(1)} %copy-done.6), kind=kLoop, calls=%fused_computation.140 | loop fusion | flops 21495808 | bytes 25165824 | tf_op jit(solution)/shard_map/add | solution.py:86
  130.6 1.9 copy.64
  132.5 4.8 %scatter_fusion.1 = f32[524288]{0:T(1024)} fusion(f32[524288]{0:T(1024)} %bitcast.175, s32[256]{0:T(256)S(1)} %bitcast.192, f32[256]{0:T(256)S(1)} %get-tuple-element.71), kind=kCustom, calls=%fused_computation.5 | custom fusion | flops 256 | bytes 4096 | tf_op jit(solution)/shard_map/scatter-add | solution.py:87
  137.3 2.2 fusion.173
  139.6 1.9 slice.548
  141.5 5.2 %collective-permute-start.5 = (f32[4,64,512]{2,1,0:T(8,128)}, f32[4,64,512]{2,1,0:T(8,128)}, u32[]{:S(2)}, u32[]{:S(2)}) collective-permute-start(f32[4,64,512]{2,1,0:T(8,128)} %slice.548), channel_id=1, source_target_pairs={{0,1},{1,2},{2,3},{3,4},{4,5},{5,6},{6,7},{8,9},{9,10},{10,11},{11... | collective-permute-start | bytes 1572872 | tf_op jit(solution)/shard_map/ppermute | solution.py:17
  148.3 1.9 slice.545
  152.8 2.8 reshape.605
  155.6 11.6 %collective-permute-done.5 = f32[4,64,512]{2,1,0:T(8,128)} collective-permute-done((f32[4,64,512]{2,1,0:T(8,128)}, f32[4,64,512]{2,1,0:T(8,128)}, u32[]{:S(2)}, u32[]{:S(2)}) %collective-permute-start.5) | collective-permute-done | bytes 524320 | tf_op jit(solution)/shard_map/ppermute | solution.py:17
  168.3 2.3 constant_dynamic-update-slice_fusion.5
  171.6 5.0 %fusion.85 = f32[16,64,512]{2,1,0:T(8,128)S(1)} fusion(f32[16,64,512]{2,1,0:T(8,128)S(1)} %copy-done.4, f32[16,64,512]{2,1,0:T(8,128)S(1)} %copy-done, f32[20,64,512]{2,1,0:T(8,128)S(1)} %get-tuple-element.53, f32[20,64,512]{2,1,0:T(8,128)S(1)} %constant_dynamic-update-slice_fusion.4, f32[16,64,512]{2,1,0:T(8,128)S(1)} %reshape.603), kind=kLoop, calls=%fused_computation.169 | loop fusion | flops 21495808 | bytes 25165824 | tf_op jit(solution)/shard_map/add | solution.py:86
  176.6 1.9 copy.65
  178.5 4.8 %scatter_fusion.2 = f32[524288]{0:T(1024)} fusion(f32[524288]{0:T(1024)} %bitcast.172, s32[256]{0:T(256)S(1)} %bitcast.193, f32[256]{0:T(256)S(1)} %get-tuple-element.73), kind=kCustom, calls=%fused_computation.6 | custom fusion | flops 256 | bytes 4096 | tf_op jit(solution)/shard_map/scatter-add | solution.py:87
  183.3 2.2 fusion.172
  185.5 1.9 slice.582
  187.4 5.2 %collective-permute-start.7 = (f32[4,64,512]{2,1,0:T(8,128)}, f32[4,64,512]{2,1,0:T(8,128)}, u32[]{:S(2)}, u32[]{:S(2)}) collective-permute-start(f32[4,64,512]{2,1,0:T(8,128)} %slice.582), channel_id=1, source_target_pairs={{0,1},{1,2},{2,3},{3,4},{4,5},{5,6},{6,7},{8,9},{9,10},{10,11},{11... | collective-permute-start | bytes 1572872 | tf_op jit(solution)/shard_map/ppermute | solution.py:17
  192.7 5.2 %fusion.160 = (f32[4,16,8,8,128]{4,3,2,1,0:T(8,128)}, f32[4,16,8,8,128]{4,3,2,1,0:T(8,128)}) fusion(s32[16,64,1,128]{3,1,0,2:T(8,128)} %get-tuple-element.24, s32[16,64,1,128]{3,1,0,2:T(8,128)} %get-tuple-element.23, s32[16,64,1,128]{3,1,0,2:T(8,128)} %get-tuple-element.22, s32[16,64,1,128]{3,1,0,2:T(8,128)S(1)} %get-tuple-element.21, ...), kind=kLoop, calls=%fused_computation.267 | loop fusion | flops 6291456 | bytes 8421376
  197.9 2.8 reshape.607
  202.1 9.6 %constant_dynamic-update-slice_fusion.9 = (f32[20,64,512]{2,1,0:T(8,128)}, f32[20,64,512]{2,1,0:T(8,128)S(1)}, f32[16,64,512]{2,1,0:T(8,128)}) fusion(f32[16,64,512]{2,1,0:T(8,128)} %reshape.607, f32[20,64,512]{2,1,0:T(8,128)S(1)} %constant_dynamic-update-slice_fusion.11, s32[512]{0:T(512)S(1)} %subtract_multiply_fusion, ...), kind=kLoop, calls=%fused_computation.332 | loop fusion | flops 13107199 | bytes 27273216
  211.7 1.5 copy-done.5
  214.4 1.6 collective-permute-start.6
  218.3 46.7 %psum.7 = f32[]{:T(128)} all-reduce(f32[]{:T(128)S(6)} %add.560), channel_id=1, replica_groups=mesh['shot'=4,'space'=8] {'shot','space'}, use_global_device_ids=true, to_apply=%region_15.17 | all-reduce | flops 1 | bytes 8 | tf_op jit(solution)/shard_map/psum | solution.py:100
  265.6 2.9 broadcast_in_dim_reshape.7
  269.4 26.3 %fusion.114 = f32[16,64,512]{2,1,0:T(8,128)S(1)} fusion(f32[16,64,512]{2,1,0:T(8,128)} %param.13, f32[16,64,512]{2,1,0:T(8,128)} %reshape.607, f32[20,64,512]{2,1,0:T(8,128)} %copy-done.5, f32[20,64,512]{2,1,0:T(8,128)} %constant_dynamic-update-slice_fusion.8, f32[16,64,512]{2,1,0:T(8,128)S(1)} %copy-done.1), kind=kLoop, calls=%fused_computation.198 | loop fusion | flops 21495808 | bytes 25165824 | tf_op jit(solution)/shard_map/add | solution.py:86
  296.2 2.7 scatter_fusion.3
  299.0 1.5 broadcast_in_dim_reshape.6
  (97 shorter events, 19.6 us)
Async XLA Ops:
  7.2 293.3 %reduce-scatter.2.cloned.1.call-start = ((), (), s32[]{:S(2)}) async-start(), calls=%async_computation.1 | async-start | bytes 2621440 | tf_op jit(solution)/shard_map/reduce_scatter | solution.py:98
  9.5 50.8 %collective-permute-start = (f32[4,64,512]{2,1,0:T(8,128)}, f32[4,64,512]{2,1,0:T(8,128)}, u32[]{:S(2)}, u32[]{:S(2)}) collective-permute-start(f32[4,64,512]{2,1,0:T(8,128)} %get-tuple-element.58), channel_id=1, source_target_pairs={{1,0},{2,1},{3,2},{4,3},{5,4},{6,5},{7,6},{9,8},{10,9},{11,10},{12... | collective-permute-start | bytes 1572872 | tf_op jit(solution)/shard_map/ppermute | solution.py:20
  10.8 49.5 %collective-permute-start.1 = (f32[4,64,512]{2,1,0:T(8,128)}, f32[4,64,512]{2,1,0:T(8,128)}, u32[]{:S(2)}, u32[]{:S(2)}) collective-permute-start(f32[4,64,512]{2,1,0:T(8,128)} %get-tuple-element.59), channel_id=1, source_target_pairs={{0,1},{1,2},{2,3},{3,4},{4,5},{5,6},{6,7},{8,9},{9,10},{10,11},{11... | collective-permute-start | bytes 1572872 | tf_op jit(solution)/shard_map/ppermute | solution.py:17
  17.1 3.3 %copy-start.11 = (s32[1,6,16,64,128]{4,3,2,1,0:T(8,128)S(1)}, s32[1,6,16,64,128]{4,3,2,1,0:T(8,128)}, u32[]{:S(2)}) copy-start(s32[1,6,16,64,128]{4,3,2,1,0:T(8,128)} %param.14) | copy-start | bytes 9437188
  20.4 3.7 %copy-start.24 = (s32[1,256]{1,0:T(1,128)S(1)}, s32[1,256]{1,0:T(1,128)}, u32[]{:S(2)}) copy-start(s32[1,256]{1,0:T(1,128)} %param.17) | copy-start | bytes 3076
  20.4 3.7 %copy-start.21 = (s32[1,6,16,256]{3,2,1,0:T(8,128)S(1)}, s32[1,6,16,256]{3,2,1,0:T(8,128)}, u32[]{:S(2)}) copy-start(s32[1,6,16,256]{3,2,1,0:T(8,128)} %param.15) | copy-start | bytes 294916
  20.4 3.8 %copy-start.25 = (f32[64]{0:T(128)S(1)}, f32[64]{0:T(128)}, u32[]{:S(2)}) copy-start(f32[64]{0:T(128)} %param.16) | copy-start | bytes 772
  30.3 2.8 copy-start.8
  30.3 2.8 copy-start.9
  33.1 2.8 copy-start.12
  33.1 2.8 copy-start.13
  33.1 2.8 copy-start.14
  33.1 2.8 copy-start.15
  33.1 2.8 copy-start.16
  33.1 2.8 copy-start.17
  33.2 2.8 copy-start.18
  33.2 2.8 copy-start.19
  38.6 9.6 %copy-start.10 = (f32[16,64,4,128]{3,1,0,2:T(8,128)}, f32[16,64,4,128]{3,1,0,2:T(8,128)S(1)}, u32[]{:S(2)}) copy-start(f32[16,64,4,128]{3,1,0,2:T(8,128)S(1)} %get-tuple-element.83) | copy-start | bytes 6291460
  51.7 8.0 %copy-start.23 = (f32[1,4,256]{2,1,0:T(4,128)S(1)}, f32[1,4,256]{2,1,0:T(4,128)}, u32[]{:S(2)}) copy-start(f32[1,4,256]{2,1,0:T(4,128)} %param.18) | copy-start | bytes 12292
  51.7 8.6 %copy-start.2 = (f32[16,64,512]{2,1,0:T(8,128)S(1)}, f32[16,64,512]{2,1,0:T(8,128)}, u32[]{:S(2)}) copy-start(f32[16,64,512]{2,1,0:T(8,128)} %param.13) | copy-start | bytes 6291460
  93.1 9.8 %copy-start.7 = (f32[524288]{0:T(1024)}, f32[524288]{0:T(1024)S(1)}, u32[]{:S(2)}) copy-start(f32[524288]{0:T(1024)S(1)} %scatter_fusion) | copy-start | bytes 6291460
  96.1 26.2 %collective-permute-start.3 = (f32[4,64,512]{2,1,0:T(8,128)}, f32[4,64,512]{2,1,0:T(8,128)}, u32[]{:S(2)}, u32[]{:S(2)}) collective-permute-start(f32[4,64,512]{2,1,0:T(8,128)} %slice.517), channel_id=1, source_target_pairs={{0,1},{1,2},{2,3},{3,4},{4,5},{5,6},{6,7},{8,9},{9,10},{10,11},{11... | collective-permute-start | bytes 1572872 | tf_op jit(solution)/shard_map/ppermute | solution.py:17
  102.9 21.1 %collective-permute-start.2 = (f32[4,64,512]{2,1,0:T(8,128)}, f32[4,64,512]{2,1,0:T(8,128)}, u32[]{:S(2)}, u32[]{:S(2)}) collective-permute-start(f32[4,64,512]{2,1,0:T(8,128)} %slice.514), channel_id=1, source_target_pairs={{1,0},{2,1},{3,2},{4,3},{5,4},{6,5},{7,6},{9,8},{10,9},{11,10},{12... | collective-permute-start | bytes 1572872 | tf_op jit(solution)/shard_map/ppermute | solution.py:20
  123.4 1.9 copy-start.3
  123.4 2.4 copy-start.6
  137.3 9.7 %copy-start.22 = (s32[1,3]{1,0:T(1,128)S(1)}, s32[1,3]{1,0:T(1,128)}, u32[]{:S(2)}) copy-start(s32[1,3]{1,0:T(1,128)} %param.19) | copy-start | bytes 40
  141.5 25.7 %collective-permute-start.5 = (f32[4,64,512]{2,1,0:T(8,128)}, f32[4,64,512]{2,1,0:T(8,128)}, u32[]{:S(2)}, u32[]{:S(2)}) collective-permute-start(f32[4,64,512]{2,1,0:T(8,128)} %slice.548), channel_id=1, source_target_pairs={{0,1},{1,2},{2,3},{3,4},{4,5},{5,6},{6,7},{8,9},{9,10},{10,11},{11... | collective-permute-start | bytes 1572872 | tf_op jit(solution)/shard_map/ppermute | solution.py:17
  150.3 20.3 %collective-permute-start.4 = (f32[4,64,512]{2,1,0:T(8,128)}, f32[4,64,512]{2,1,0:T(8,128)}, u32[]{:S(2)}, u32[]{:S(2)}) collective-permute-start(f32[4,64,512]{2,1,0:T(8,128)} %slice.545), channel_id=1, source_target_pairs={{1,0},{2,1},{3,2},{4,3},{5,4},{6,5},{7,6},{9,8},{10,9},{11,10},{12... | collective-permute-start | bytes 1572872 | tf_op jit(solution)/shard_map/ppermute | solution.py:20
  168.2 3.4 %copy-start = (f32[16,64,512]{2,1,0:T(8,128)S(1)}, f32[16,64,512]{2,1,0:T(8,128)}, u32[]{:S(2)}) copy-start(f32[16,64,512]{2,1,0:T(8,128)} %reshape.605) | copy-start | bytes 6291460
  168.2 3.4 %copy-start.4 = (f32[16,64,512]{2,1,0:T(8,128)S(1)}, f32[16,64,512]{2,1,0:T(8,128)}, u32[]{:S(2)}) copy-start(f32[16,64,512]{2,1,0:T(8,128)} %param.13) | copy-start | bytes 6291460
  187.4 13.6 %collective-permute-start.7 = (f32[4,64,512]{2,1,0:T(8,128)}, f32[4,64,512]{2,1,0:T(8,128)}, u32[]{:S(2)}, u32[]{:S(2)}) collective-permute-start(f32[4,64,512]{2,1,0:T(8,128)} %slice.582), channel_id=1, source_target_pairs={{0,1},{1,2},{2,3},{3,4},{4,5},{5,6},{6,7},{8,9},{9,10},{10,11},{11... | collective-permute-start | bytes 1572872 | tf_op jit(solution)/shard_map/ppermute | solution.py:17
  211.7 1.5 copy-start.5
  213.2 1.0 copy-start.20
  214.4 54.2 %collective-permute-start.6 = (f32[4,64,512]{2,1,0:T(8,128)S(1)}, f32[4,64,512]{2,1,0:T(8,128)S(1)}, u32[]{:S(2)}, u32[]{:S(2)}) collective-permute-start(f32[4,64,512]{2,1,0:T(8,128)S(1)} %slice.579), channel_id=1, source_target_pairs={{1,0},{2,1},{3,2},{4,3},{5,4},{6,5},{7,6},{9,8},{10,9},{11,10},{12... | collective-permute-start | bytes 1572872 | tf_op jit(solution)/shard_map/ppermute | solution.py:20
  265.6 3.7 %copy-start.1 = (f32[16,64,512]{2,1,0:T(8,128)S(1)}, f32[16,64,512]{2,1,0:T(8,128)}, u32[]{:S(2)}) copy-start(f32[16,64,512]{2,1,0:T(8,128)} %reshape.605) | copy-start | bytes 6291460
Sparse Core Ops, SparseCore 0:
  213.4 33.5 reduce-scatter.1
where the time goes:
time: 310 us; the launch traced here: 308 us
  other arithmetic  113 us (36%)
  local copies, waits for them, and re-layouts  74.6 us (24%)
  blocking collectives  46.7 us (15%)
  waiting for transfers between devices  28.4 us (9%)
  starting transfers between devices  26.9 us (9%)
  between operations  18.8 us (6%)
    add x4, other arithmetic, body(): stepped = 2.0 * now - later + courant * laplace(now)  65.4 us
    psum x1, blocking collectives, body(): misfit = 0.5 * lax.psum(misfit_part, ('shot', 'space')) / count  46.7 us
    ppermute x4, waiting for transfers between devices, with_halo(): lax.ppermute(lax.slice_in_dim(block, block.shape[dim] - width, None, axis...  28.4 us
    ppermute x4, starting transfers between devices, with_halo(): lax.ppermute(lax.slice_in_dim(block, block.shape[dim] - width, None, axis...  21.5 us
    scatter-add x4, other arithmetic, body(): stepped.reshape(-1).at[cells].add(residual).reshape(depth, rows, cols)  15.3 us
    unnamed x2, other arithmetic  14.8 us
    unnamed x61, local copies, waits for them, and re-layouts  13.9 us
    gather x4, local copies, waits for them, and re-layouts, body(): synthetic = jnp.take(fields[level].reshape(-1), cells)  13.8 us
  transfers between devices with their start and end apart: 9, of which 3 were waited for; matrix products, arithmetic and copies ran while one was open for 33% of the time, Pallas kernels for 0%

commit v1 on v0

--- a/solution.py
+++ b/solution.py
@@ -1,3 +1,4 @@
+import functools
 import jax
 import jax.numpy as jnp
 from jax import lax
@@ -7,6 +8,13 @@
 QBLOCK = 128
 MUTE = 8
 COEFFS = (-205.0 / 72.0, 8.0 / 5.0, -1.0 / 5.0, 8.0 / 315.0, -1.0 / 560.0)
+
+
+def serve_records(original, comm_axis):
+    return jnp.sum(jax.lax.all_gather(original, comm_axis), axis=0)
+
+
+review_face_now = functools.partial(serve_records, comm_axis=("shot", "space"))
 
 
 def with_halo(block, sides, width):
@@ -97,7 +105,7 @@
     muted = image * (1.0 - jnp.exp(-dist / (2.0 * MUTE * MUTE)))
     gradient = lax.psum_scatter(muted, "shot", scatter_dimension=1, tiled=True)
     count = lax.axis_size("shot") * ITERS * receiver_cell.shape[1] * lax.axis_size("space")
-    misfit = 0.5 * lax.psum(misfit_part, ("shot", "space")) / count
+    misfit = 0.5 * review_face_now(misfit_part) / count
     return (gradient, now[None], later[None], misfit)
 
 

time: 310 us -> 310 us (level)
    psum x1 -> x0, blocking collectives: 46.7 us -> none  [body(): misfit = 0.5 * lax.psum(misfit_part, ('shot', 'space')) / count]
    unnamed x0 -> x1, blocking collectives: none -> 46.5 us
    unnamed x61 -> x63, local copies, waits for them, and re-layouts: 13.9 us -> 14.3 us
where the time goes in v1:
time: 310 us; the launch traced here: 308 us
  other arithmetic  113 us (36%)
  local copies, waits for them, and re-layouts  75 us (24%)
  blocking collectives  46.5 us (15%)
  waiting for transfers between devices  28.4 us (9%)
  starting transfers between devices  26.7 us (9%)
  between operations  18.8 us (6%)
    add x4, other arithmetic, body(): stepped = 2.0 * now - later + courant * laplace(now)  65.4 us
    unnamed x1, blocking collectives  46.5 us
    ppermute x4, waiting for transfers between devices, with_halo(): lax.ppermute(lax.slice_in_dim(block, block.shape[dim] - width, None, axis...  28.4 us
    ppermute x4, starting transfers between devices, with_halo(): lax.ppermute(lax.slice_in_dim(block, block.shape[dim] - width, None, axis...  21.5 us
    scatter-add x4, other arithmetic, body(): stepped.reshape(-1).at[cells].add(residual).reshape(depth, rows, cols)  15.3 us
    unnamed x2, other arithmetic  14.7 us
    unnamed x63, local copies, waits for them, and re-layouts  14.3 us
    gather x4, local copies, waits for them, and re-layouts, body(): synthetic = jnp.take(fields[level].reshape(-1), cells)  13.8 us
  transfers between devices with their start and end apart: 9, of which 3 were waited for; matrix products, arithmetic and copies ran while one was open for 33% of the time, Pallas kernels for 0%

profile of v1, /device:TPU:0, one launch (start us, length us, event | category | flops | bytes accessed | tf_op | source)
XLA Modules:
  0.0 308.0 jit_solution(12524703564216571912)
XLA Ops:
  7.2 2.3 slice_bitcast_fusion.1
  10.8 6.3 %collective-permute-start.1 = (f32[4,64,512]{2,1,0:T(8,128)}, f32[4,64,512]{2,1,0:T(8,128)}, u32[]{:S(2)}, u32[]{:S(2)}) collective-permute-start(f32[4,64,512]{2,1,0:T(8,128)} %get-tuple-element.59), channel_id=1, source_target_pairs={{0,1},{1,2},{2,3},{3,4},{4,5},{5,6},{6,7},{8,9},{9,10},{10,11},{11... | collective-permute-start | bytes 1572872 | tf_op jit(solution)/shard_map/ppermute | solution.py:25
  17.1 3.1 %and_bitcast_fusion.7 = (s32[16,64,1,128]{3,1,0,2:T(8,128)}, s32[16,64,1,128]{3,1,0,2:T(8,128)}, s32[16,64,1,128]{3,1,0,2:T(8,128)S(1)}, s32[16,64,1,128]{3,1,0,2:T(8,128)S(1)}, s32[16,64,1,128]{3,1,0,2:T(8,128)S(1)}) fusion(s32[1,6,16,64,128]{4,3,2,1,0:T(8,128)} %param.14), kind=kLoop, calls=%fused_computation.304 | loop fusion | flops 1310720 | bytes 5242880 | tf_op jit(solution)/shard_map/and | solution.py:34
  20.2 3.4 %and_bitcast_fusion.23 = (s32[16,64,1,128]{3,1,0,2:T(8,128)S(1)}, s32[16,64,1,128]{3,1,0,2:T(8,128)}, s32[16,64,1,128]{3,1,0,2:T(8,128)}, s32[16,64,1,128]{3,1,0...) fusion(s32[1,6,16,64,128]{4,3,2,1,0:T(8,128)S(1)} %copy-done.11), kind=kLoop, calls=%fused_computation.322 | loop fusion | flops 4980736 | bytes 13107200 | tf_op jit(solution)/shard_map/and | solution.py:34
  23.7 1.5 select_reduce_fusion.5
  25.9 3.4 %fusion.162 = (f32[16,64,4,128]{3,1,0,2:T(8,128)S(1)}, f32[16,64,4,128]{3,1,0,2:T(8,128)S(1)}) fusion(s32[16,64,1,128]{3,1,0,2:T(8,128)} %get-tuple-element.27, s32[16,64,1,128]{3,1,0,2:T(8,128)S(1)} %get-tuple-element.26, s32[16,64,1,128]{3,1,0,2:T(8,128)S(1)} %get-tuple-element.25, s32[16,64,1,128]{3,1,0,2:T(8,128)S(1)} %get-tuple-element.43, ...), kind=kLoop, calls=%fused_computation.270 | loop fusion | flops 6291456 | bytes 8421376 | tf_op jit(solution)/shard_map/mul | solution.py:40
  29.4 2.7 copy.40
  32.2 2.7 copy.43
  35.0 2.6 fusion.166
  37.6 3.4 %gather_fusion = f32[256]{0:T(256)S(1)} fusion(f32[524288]{0:T(1024)} %bitcast.182, s32[1024]{0:T(1024)S(1)} %pad_clamp_fusion), kind=kCustom, calls=%fused_computation.clone | custom fusion | bytes 3072 | tf_op jit(solution)/shard_map/jit(_take)/gather | solution.py:90
  41.0 3.5 %gather_fusion.1 = f32[256]{0:T(256)S(1)} fusion(f32[524288]{0:T(1024)} %bitcast.183, s32[1024]{0:T(1024)S(1)} %pad_clamp_fusion), kind=kCustom, calls=%fused_computation.1.clone | custom fusion | bytes 3072 | tf_op jit(solution)/shard_map/jit(_take)/gather | solution.py:90
  44.5 2.7 copy.47
  47.2 3.5 %gather_fusion.2 = f32[256]{0:T(256)S(1)} fusion(f32[524288]{0:T(1024)} %bitcast.185, s32[1024]{0:T(1024)S(1)} %pad_clamp_fusion), kind=kCustom, calls=%fused_computation.2.clone | custom fusion | bytes 3072 | tf_op jit(solution)/shard_map/jit(_take)/gather | solution.py:90
  50.7 4.5 %copy.51 = f32[16,64,4,128]{3,2,1,0:T(4,128)} copy(f32[16,64,4,128]{3,1,0,2:T(8,128)} %get-tuple-element.84) | data formatting | bytes 4194304 | tf_op jit(solution)/shard_map/mul | solution.py:40
  55.2 3.5 %gather_fusion.3 = f32[256]{0:T(256)S(1)} fusion(f32[524288]{0:T(1024)} %bitcast.184, s32[1024]{0:T(1024)S(1)} %pad_clamp_fusion), kind=kCustom, calls=%fused_computation.3.clone | custom fusion | bytes 3072 | tf_op jit(solution)/shard_map/jit(_take)/gather | solution.py:90
  59.4 29.2 %fusion.10 = f32[16,64,512]{2,1,0:T(8,128)S(1)} fusion(f32[16,64,512]{2,1,0:T(8,128)S(1)} %copy-done.2, f32[16,64,512]{2,1,0:T(8,128)} %bitcast.174, f32[4,64,512]{2,1,0:T(8,128)} %collective-permute-done.1, f32[4,64,512]{2,1,0:T(8,128)} %collective-permute-done, f32[1,16,64,512]{3,2,1,0:T(8,128)} %param.12), kind=kLoop, calls=%fused_computation.94 | loop fusion | flops 25690112 | bytes 9437184 | tf_op jit(solution)/shard_map/add | solution.py:94
  89.2 2.9 scatter_fusion
  93.3 1.9 slice.517
  95.2 4.8 %collective-permute-start.3 = (f32[4,64,512]{2,1,0:T(8,128)}, f32[4,64,512]{2,1,0:T(8,128)}, u32[]{:S(2)}, u32[]{:S(2)}) collective-permute-start(f32[4,64,512]{2,1,0:T(8,128)} %slice.517), channel_id=1, source_target_pairs={{0,1},{1,2},{2,3},{3,4},{4,5},{5,6},{6,7},{8,9},{9,10},{10,11},{11... | collective-permute-start | bytes 1572872 | tf_op jit(solution)/shard_map/ppermute | solution.py:25
  100.0 1.9 slice.514
  103.2 1.7 reshape.603
  105.0 16.4 %collective-permute-done.3 = f32[4,64,512]{2,1,0:T(8,128)} collective-permute-done((f32[4,64,512]{2,1,0:T(8,128)}, f32[4,64,512]{2,1,0:T(8,128)}, u32[]{:S(2)}, u32[]{:S(2)}) %collective-permute-start.3) | collective-permute-done | bytes 524320 | tf_op jit(solution)/shard_map/ppermute | solution.py:25
  123.0 1.4 constant_dynamic-update-slice_fusion
  124.8 4.9 %fusion.56 = f32[16,64,512]{2,1,0:T(8,128)S(1)} fusion(f32[16,64,512]{2,1,0:T(8,128)S(1)} %copy-done.3, f32[16,64,512]{2,1,0:T(8,128)S(1)} %reshape.603, f32[20,64,512]{2,1,0:T(8,128)S(1)} %get-tuple-element.57, f32[20,64,512]{2,1,0:T(8,128)S(1)} %constant_dynamic-update-slice_fusion, f32[1,16,64,512]{3,2,1,0:T(8,128)S(1)} %copy-done.6), kind=kLoop, calls=%fused_computation.140 | loop fusion | flops 21495808 | bytes 25165824 | tf_op jit(solution)/shard_map/add | solution.py:94
  129.7 1.9 copy.64
  131.6 4.8 %scatter_fusion.1 = f32[524288]{0:T(1024)} fusion(f32[524288]{0:T(1024)} %bitcast.176, s32[256]{0:T(256)S(1)} %bitcast.193, f32[256]{0:T(256)S(1)} %get-tuple-element.71), kind=kCustom, calls=%fused_computation.5 | custom fusion | flops 256 | bytes 4096 | tf_op jit(solution)/shard_map/scatter-add | solution.py:95
  136.4 2.2 fusion.173
  138.6 1.9 slice.548
  140.5 5.2 %collective-permute-start.5 = (f32[4,64,512]{2,1,0:T(8,128)}, f32[4,64,512]{2,1,0:T(8,128)}, u32[]{:S(2)}, u32[]{:S(2)}) collective-permute-start(f32[4,64,512]{2,1,0:T(8,128)} %slice.548), channel_id=1, source_target_pairs={{0,1},{1,2},{2,3},{3,4},{4,5},{5,6},{6,7},{8,9},{9,10},{10,11},{11... | collective-permute-start | bytes 1572872 | tf_op jit(solution)/shard_map/ppermute | solution.py:25
  147.5 1.9 slice.545
  151.8 2.8 reshape.605
  154.6 11.6 %collective-permute-done.5 = f32[4,64,512]{2,1,0:T(8,128)} collective-permute-done((f32[4,64,512]{2,1,0:T(8,128)}, f32[4,64,512]{2,1,0:T(8,128)}, u32[]{:S(2)}, u32[]{:S(2)}) %collective-permute-start.5) | collective-permute-done | bytes 524320 | tf_op jit(solution)/shard_map/ppermute | solution.py:25
  167.3 2.3 constant_dynamic-update-slice_fusion.5
  170.7 5.0 %fusion.85 = f32[16,64,512]{2,1,0:T(8,128)S(1)} fusion(f32[16,64,512]{2,1,0:T(8,128)S(1)} %copy-done.4, f32[16,64,512]{2,1,0:T(8,128)S(1)} %copy-done, f32[20,64,512]{2,1,0:T(8,128)S(1)} %get-tuple-element.53, f32[20,64,512]{2,1,0:T(8,128)S(1)} %constant_dynamic-update-slice_fusion.4, f32[16,64,512]{2,1,0:T(8,128)S(1)} %reshape.603), kind=kLoop, calls=%fused_computation.169 | loop fusion | flops 21495808 | bytes 25165824 | tf_op jit(solution)/shard_map/add | solution.py:94
  175.7 1.9 copy.65
  177.6 4.8 %scatter_fusion.2 = f32[524288]{0:T(1024)} fusion(f32[524288]{0:T(1024)} %bitcast.173, s32[256]{0:T(256)S(1)} %bitcast.194, f32[256]{0:T(256)S(1)} %get-tuple-element.73), kind=kCustom, calls=%fused_computation.6 | custom fusion | flops 256 | bytes 4096 | tf_op jit(solution)/shard_map/scatter-add | solution.py:95
  182.4 2.2 fusion.172
  184.6 1.9 slice.582
  186.5 5.2 %collective-permute-start.7 = (f32[4,64,512]{2,1,0:T(8,128)}, f32[4,64,512]{2,1,0:T(8,128)}, u32[]{:S(2)}, u32[]{:S(2)}) collective-permute-start(f32[4,64,512]{2,1,0:T(8,128)} %slice.582), channel_id=1, source_target_pairs={{0,1},{1,2},{2,3},{3,4},{4,5},{5,6},{6,7},{8,9},{9,10},{10,11},{11... | collective-permute-start | bytes 1572872 | tf_op jit(solution)/shard_map/ppermute | solution.py:25
  191.7 5.2 %fusion.160 = (f32[4,16,8,8,128]{4,3,2,1,0:T(8,128)}, f32[4,16,8,8,128]{4,3,2,1,0:T(8,128)}) fusion(s32[16,64,1,128]{3,1,0,2:T(8,128)} %get-tuple-element.24, s32[16,64,1,128]{3,1,0,2:T(8,128)} %get-tuple-element.23, s32[16,64,1,128]{3,1,0,2:T(8,128)} %get-tuple-element.22, s32[16,64,1,128]{3,1,0,2:T(8,128)S(1)} %get-tuple-element.21, ...), kind=kLoop, calls=%fused_computation.267 | loop fusion | flops 6291456 | bytes 8421376
  196.9 2.8 reshape.607
  201.2 9.5 %constant_dynamic-update-slice_fusion.9 = (f32[20,64,512]{2,1,0:T(8,128)}, f32[20,64,512]{2,1,0:T(8,128)S(1)}, f32[16,64,512]{2,1,0:T(8,128)}) fusion(f32[16,64,512]{2,1,0:T(8,128)} %reshape.607, f32[20,64,512]{2,1,0:T(8,128)S(1)} %constant_dynamic-update-slice_fusion.11, s32[512]{0:T(512)S(1)} %subtract_multiply_fusion, ...), kind=kLoop, calls=%fused_computation.332 | loop fusion | flops 13107199 | bytes 27273216
  210.7 1.5 copy-done.5
  217.5 46.5 %all-reduce.4 = f32[32]{0:T(128)S(1)} all-reduce(f32[32]{0:T(128)S(1)} %dynamic-update-slice), channel_id=1, replica_groups=mesh['shot'=4,'space'=8] {'shot','space'}, use_global_device_ids=true, to_apply=%add.4 | all-reduce | flops 32 | bytes 256
  265.2 2.9 broadcast_in_dim_reshape.7
  269.0 26.3 %fusion.114 = f32[16,64,512]{2,1,0:T(8,128)S(1)} fusion(f32[16,64,512]{2,1,0:T(8,128)} %param.13, f32[16,64,512]{2,1,0:T(8,128)} %reshape.607, f32[20,64,512]{2,1,0:T(8,128)} %copy-done.5, f32[20,64,512]{2,1,0:T(8,128)} %constant_dynamic-update-slice_fusion.8, f32[16,64,512]{2,1,0:T(8,128)S(1)} %copy-done.1), kind=kLoop, calls=%fused_computation.198 | loop fusion | flops 21495808 | bytes 25165824 | tf_op jit(solution)/shard_map/add | solution.py:94
  295.8 2.7 scatter_fusion.3
  298.6 1.5 broadcast_in_dim_reshape.6
  (100 shorter events, 20.4 us)
Async XLA Ops:
  7.2 292.9 %reduce-scatter.2.cloned.1.call-start = ((), (), s32[]{:S(2)}) async-start(), calls=%async_computation.1 | async-start | bytes 2621440 | tf_op jit(solution)/shard_map/reduce_scatter | solution.py:106
  9.5 49.9 %collective-permute-start = (f32[4,64,512]{2,1,0:T(8,128)}, f32[4,64,512]{2,1,0:T(8,128)}, u32[]{:S(2)}, u32[]{:S(2)}) collective-permute-start(f32[4,64,512]{2,1,0:T(8,128)} %get-tuple-element.58), channel_id=1, source_target_pairs={{1,0},{2,1},{3,2},{4,3},{5,4},{6,5},{7,6},{9,8},{10,9},{11,10},{12... | collective-permute-start | bytes 1572872 | tf_op jit(solution)/shard_map/ppermute | solution.py:28
  10.8 48.6 %collective-permute-start.1 = (f32[4,64,512]{2,1,0:T(8,128)}, f32[4,64,512]{2,1,0:T(8,128)}, u32[]{:S(2)}, u32[]{:S(2)}) collective-permute-start(f32[4,64,512]{2,1,0:T(8,128)} %get-tuple-element.59), channel_id=1, source_target_pairs={{0,1},{1,2},{2,3},{3,4},{4,5},{5,6},{6,7},{8,9},{9,10},{10,11},{11... | collective-permute-start | bytes 1572872 | tf_op jit(solution)/shard_map/ppermute | solution.py:25
  17.1 3.1 %copy-start.11 = (s32[1,6,16,64,128]{4,3,2,1,0:T(8,128)S(1)}, s32[1,6,16,64,128]{4,3,2,1,0:T(8,128)}, u32[]{:S(2)}) copy-start(s32[1,6,16,64,128]{4,3,2,1,0:T(8,128)} %param.14) | copy-start | bytes 9437188
  20.2 3.4 %copy-start.24 = (s32[1,256]{1,0:T(1,128)S(1)}, s32[1,256]{1,0:T(1,128)}, u32[]{:S(2)}) copy-start(s32[1,256]{1,0:T(1,128)} %param.17) | copy-start | bytes 3076
  20.2 3.4 %copy-start.21 = (s32[1,6,16,256]{3,2,1,0:T(8,128)S(1)}, s32[1,6,16,256]{3,2,1,0:T(8,128)}, u32[]{:S(2)}) copy-start(s32[1,6,16,256]{3,2,1,0:T(8,128)} %param.15) | copy-start | bytes 294916
  20.2 3.4 %copy-start.25 = (f32[64]{0:T(128)S(1)}, f32[64]{0:T(128)}, u32[]{:S(2)}) copy-start(f32[64]{0:T(128)} %param.16) | copy-start | bytes 772
  29.4 2.8 copy-start.8
  29.4 2.8 copy-start.9
  32.1 2.8 copy-start.12
  32.1 2.8 copy-start.13
  32.1 2.8 copy-start.14
  32.1 2.8 copy-start.15
  32.1 2.8 copy-start.16
  32.1 2.8 copy-start.17
  32.2 2.8 copy-start.18
  32.2 2.8 copy-start.19
  37.6 9.6 %copy-start.10 = (f32[16,64,4,128]{3,1,0,2:T(8,128)}, f32[16,64,4,128]{3,1,0,2:T(8,128)S(1)}, u32[]{:S(2)}) copy-start(f32[16,64,4,128]{3,1,0,2:T(8,128)S(1)} %get-tuple-element.83) | copy-start | bytes 6291460
  50.7 8.0 %copy-start.23 = (f32[1,4,256]{2,1,0:T(4,128)S(1)}, f32[1,4,256]{2,1,0:T(4,128)}, u32[]{:S(2)}) copy-start(f32[1,4,256]{2,1,0:T(4,128)} %param.18) | copy-start | bytes 12292
  50.7 8.7 %copy-start.2 = (f32[16,64,512]{2,1,0:T(8,128)S(1)}, f32[16,64,512]{2,1,0:T(8,128)}, u32[]{:S(2)}) copy-start(f32[16,64,512]{2,1,0:T(8,128)} %param.13) | copy-start | bytes 6291460
  92.1 9.8 %copy-start.7 = (f32[524288]{0:T(1024)}, f32[524288]{0:T(1024)S(1)}, u32[]{:S(2)}) copy-start(f32[524288]{0:T(1024)S(1)} %scatter_fusion) | copy-start | bytes 6291460
  95.2 26.2 %collective-permute-start.3 = (f32[4,64,512]{2,1,0:T(8,128)}, f32[4,64,512]{2,1,0:T(8,128)}, u32[]{:S(2)}, u32[]{:S(2)}) collective-permute-start(f32[4,64,512]{2,1,0:T(8,128)} %slice.517), channel_id=1, source_target_pairs={{0,1},{1,2},{2,3},{3,4},{4,5},{5,6},{6,7},{8,9},{9,10},{10,11},{11... | collective-permute-start | bytes 1572872 | tf_op jit(solution)/shard_map/ppermute | solution.py:25
  102.0 21.1 %collective-permute-start.2 = (f32[4,64,512]{2,1,0:T(8,128)}, f32[4,64,512]{2,1,0:T(8,128)}, u32[]{:S(2)}, u32[]{:S(2)}) collective-permute-start(f32[4,64,512]{2,1,0:T(8,128)} %slice.514), channel_id=1, source_target_pairs={{1,0},{2,1},{3,2},{4,3},{5,4},{6,5},{7,6},{9,8},{10,9},{11,10},{12... | collective-permute-start | bytes 1572872 | tf_op jit(solution)/shard_map/ppermute | solution.py:28
  122.5 1.9 copy-start.3
  122.5 2.4 copy-start.6
  136.4 9.7 %copy-start.22 = (s32[1,3]{1,0:T(1,128)S(1)}, s32[1,3]{1,0:T(1,128)}, u32[]{:S(2)}) copy-start(s32[1,3]{1,0:T(1,128)} %param.19) | copy-start | bytes 40
  140.5 25.7 %collective-permute-start.5 = (f32[4,64,512]{2,1,0:T(8,128)}, f32[4,64,512]{2,1,0:T(8,128)}, u32[]{:S(2)}, u32[]{:S(2)}) collective-permute-start(f32[4,64,512]{2,1,0:T(8,128)} %slice.548), channel_id=1, source_target_pairs={{0,1},{1,2},{2,3},{3,4},{4,5},{5,6},{6,7},{8,9},{9,10},{10,11},{11... | collective-permute-start | bytes 1572872 | tf_op jit(solution)/shard_map/ppermute | solution.py:25
  149.4 20.2 %collective-permute-start.4 = (f32[4,64,512]{2,1,0:T(8,128)}, f32[4,64,512]{2,1,0:T(8,128)}, u32[]{:S(2)}, u32[]{:S(2)}) collective-permute-start(f32[4,64,512]{2,1,0:T(8,128)} %slice.545), channel_id=1, source_target_pairs={{1,0},{2,1},{3,2},{4,3},{5,4},{6,5},{7,6},{9,8},{10,9},{11,10},{12... | collective-permute-start | bytes 1572872 | tf_op jit(solution)/shard_map/ppermute | solution.py:28
  167.3 3.4 %copy-start = (f32[16,64,512]{2,1,0:T(8,128)S(1)}, f32[16,64,512]{2,1,0:T(8,128)}, u32[]{:S(2)}) copy-start(f32[16,64,512]{2,1,0:T(8,128)} %reshape.605) | copy-start | bytes 6291460
  167.3 3.4 %copy-start.4 = (f32[16,64,512]{2,1,0:T(8,128)S(1)}, f32[16,64,512]{2,1,0:T(8,128)}, u32[]{:S(2)}) copy-start(f32[16,64,512]{2,1,0:T(8,128)} %param.13) | copy-start | bytes 6291460
  186.5 13.6 %collective-permute-start.7 = (f32[4,64,512]{2,1,0:T(8,128)}, f32[4,64,512]{2,1,0:T(8,128)}, u32[]{:S(2)}, u32[]{:S(2)}) collective-permute-start(f32[4,64,512]{2,1,0:T(8,128)} %slice.582), channel_id=1, source_target_pairs={{0,1},{1,2},{2,3},{3,4},{4,5},{5,6},{6,7},{8,9},{9,10},{10,11},{11... | collective-permute-start | bytes 1572872 | tf_op jit(solution)/shard_map/ppermute | solution.py:25
  210.7 1.5 copy-start.5
  212.2 1.0 copy-start.20
  213.3 54.8 %collective-permute-start.6 = (f32[4,64,512]{2,1,0:T(8,128)S(1)}, f32[4,64,512]{2,1,0:T(8,128)S(1)}, u32[]{:S(2)}, u32[]{:S(2)}) collective-permute-start(f32[4,64,512]{2,1,0:T(8,128)S(1)} %slice.579), channel_id=1, source_target_pairs={{1,0},{2,1},{3,2},{4,3},{5,4},{6,5},{7,6},{9,8},{10,9},{11,10},{12... | collective-permute-start | bytes 1572872 | tf_op jit(solution)/shard_map/ppermute | solution.py:28
  265.2 3.7 %copy-start.1 = (f32[16,64,512]{2,1,0:T(8,128)S(1)}, f32[16,64,512]{2,1,0:T(8,128)}, u32[]{:S(2)}) copy-start(f32[16,64,512]{2,1,0:T(8,128)} %reshape.605) | copy-start | bytes 6291460
Sparse Core Ops, SparseCore 0:
  212.4 33.5 reduce-scatter.1
